TPU v7x, 32 devices: a whole 2x2x4 slice. The times are simulated.
32 devices in a mesh: gx: 8 (over y, x, core), gy: 4 (over z).
Axes of the slice: x: 2, y: 2, z: 4, core: 2. Of those that a mesh axis runs over, the one named last changes fastest.
Arguments:
- layer_early: bfloat16 [1024, 8192], P(None, ('gx', 'gy')), may hold values from -48 to 48
- layer_late: bfloat16 [1024, 8192], P(('gx', 'gy')), may hold values from -48 to 48
Outputs:
- similarity: float32 [], replicated
- token_share: float32 [1024], P(('gx', 'gy'))
- early_rows: bfloat16 [1024, 8192], P(('gx', 'gy'))
- late_rows: bfloat16 [1024, 8192], P(('gx', 'gy'))
All inputs are finite; a program needn't handle non-finite values.
Results may differ from a plain program's by a relative error of at most 0.0015.
Values may be sent and summed in bfloat16 or wider, within the bound.
A program may use at most 128 MiB of HBM per device.

v0:
```python
import jax
import jax.numpy as jnp
from jax import lax
from jax.sharding import PartitionSpec as P


def pair_terms(left_early, left_late, right_early, right_late):
    dims = (((1,), (1,)), ((), ()))
    block_early = lax.dot_general(left_early, right_early, dims, preferred_element_type=jnp.float32)
    block_late = lax.dot_general(left_late, right_late, dims, preferred_element_type=jnp.float32)
    return (
        jnp.sum(block_early * block_late, axis=1),
        jnp.sum(block_early * block_early),
        jnp.sum(block_late * block_late),
    )


def body(layer_early, layer_late):
    total_rows = layer_early.shape[0]
    early_values = layer_early.astype(jnp.float32)
    early_cols = (early_values - jnp.mean(early_values, axis=0)).astype(jnp.bfloat16)
    late_values = layer_late.astype(jnp.float32)
    column_sums = lax.psum(jnp.sum(late_values, axis=0), ("gx", "gy"))
    late_rows = (late_values - column_sums / total_rows).astype(jnp.bfloat16)
    early_rows = lax.all_to_all(early_cols, ("gx", "gy"), split_axis=0, concat_axis=1, tiled=True)
    block_early, block_late = (
        lax.all_gather(early_rows, "gy", axis=0, tiled=True),
        lax.all_gather(late_rows, "gy", axis=0, tiled=True),
    )
    row_part, early_part, late_part = pair_terms(
        block_early,
        block_late,
        lax.all_gather(early_rows, "gx", axis=0, tiled=True),
        lax.all_gather(late_rows, "gx", axis=0, tiled=True),
    )
    own_align = lax.psum_scatter(row_part, "gy", scatter_dimension=0, tiled=True)
    total_kl, total_kk, total_ll = lax.psum(
        (jnp.sum(row_part), early_part, late_part), ("gx", "gy")
    )
    scale_norm = jnp.sqrt(total_kk * total_ll)
    similarity = total_kl / scale_norm
    token_share = total_rows * own_align / scale_norm
    return (similarity, token_share, early_rows, late_rows)


def solution(mesh):
    in_specs = (P(None, ("gx", "gy")), P(("gx", "gy"), None))
    out_specs = (P(), P(("gx", "gy")), P(("gx", "gy"), None), P(("gx", "gy"), None))
    return jax.shard_map(body, mesh=mesh, in_specs=in_specs, out_specs=out_specs, check_vma=False)
```

profile of v0, /device:TPU:0, one launch (start us, length us, event | category | flops | bytes accessed | tf_op | source)
XLA Modules:
  0.0 298.2 jit_solution(8457581897998979989)
XLA Ops:
  7.2 0.0 copy-start
  7.2 0.0 all-gather.9.cloned.1.call-start
  7.2 1.2 convert_reduce_fusion
  8.4 42.1 %psum.28 = f32[8192]{0:T(1024)S(1)} all-reduce(f32[8192]{0:T(1024)S(1)} %convert_reduce_fusion), channel_id=1, replica_groups=mesh['gx'=8,'gy'=4] {'gx','gy'}, use_global_device_ids=true, to_apply=%region_2.0 | all-reduce | flops 8192 | bytes 65536 | tf_op jit(solution)/shard_map/psum | solution.py:23
  50.6 1.9 fusion.1
  52.5 0.0 all-gather.9.cloned.1.call-update
  52.5 0.0 all-gather.11.cloned.1.call-start
  52.5 0.7 all-gather.11.cloned.1.call-update
  53.3 0.0 all-gather.5.cloned.1.call-start
  53.3 1.2 convert_reduce_fusion.1
  54.5 1.1 fusion
  55.6 28.2 %all_to_all.19 = bf16[32,32,256]{2,1,0:T(8,128)(2,1)S(1)} all-to-all(bf16[32,32,256]{2,1,0:T(8,128)(2,1)S(1)} %bitcast.12), channel_id=1, replica_groups=mesh['gx'=8,'gy'=4] {'gx','gy'}, dimensions={0} | all-to-all | bytes 1048576 | tf_op jit(solution)/shard_map/all_to_all | solution.py:25
  83.9 0.8 copy.8
  84.7 0.0 all-gather.5.cloned.1.call-update
  84.7 0.0 all-gather.7.cloned.1.call-start
  84.8 0.5 all-gather.7.cloned.1.call-update
  85.3 0.0 copy-done
  85.3 0.6 dynamic-slice
  86.6 22.4 %all-gather.9.cloned.1.call-done = bf16[128,8192]{1,0:T(8,128)(2,1)} async-done(((bf16[32,8192]{1,0:T(8,128)(2,1)}), bf16[128,8192]{1,0:T(8,128)(2,1)}) %all-gather.9.cloned.1.call-update) | async-done | bytes 2097168 | tf_op jit(solution)/shard_map/all_gather | solution.py:28
  109.0 38.1 %all-gather.11.cloned.1.call-done = bf16[256,8192]{1,0:T(8,128)(2,1)} async-done(((bf16[32,8192]{1,0:T(8,128)(2,1)}), bf16[256,8192]{1,0:T(8,128)(2,1)}) %all-gather.11.cloned.1.call-update) | async-done | bytes 4194320 | tf_op jit(solution)/shard_map/all_gather | solution.py:34
  147.1 4.4 %fusion.3 = f32[128,256]{1,0:T(8,128)S(1)} fusion(bf16[128,8192]{1,0:T(8,128)(2,1)} %all-gather.9.cloned.1.call-done, bf16[256,8192]{1,0:T(8,128)(2,1)} %all-gather.11.cloned.1.call-done), kind=kOutput, calls=%fused_computation.14 | convolution fusion | flops 536870912 | bytes 6422528 | tf_op jit(solution)/shard_map/dot_general | solution.py:10
  151.5 43.5 %all-gather.5.cloned.1.call-done = bf16[128,8192]{1,0:T(8,128)(2,1)} async-done(((bf16[32,8192]{1,0:T(8,128)(2,1)}), bf16[128,8192]{1,0:T(8,128)(2,1)}) %all-gather.5.cloned.1.call-update) | async-done | bytes 2097168 | tf_op jit(solution)/shard_map/all_gather | solution.py:27
  195.0 37.7 %all-gather.7.cloned.1.call-done = bf16[256,8192]{1,0:T(8,128)(2,1)} async-done(((bf16[32,8192]{1,0:T(8,128)(2,1)}), bf16[256,8192]{1,0:T(8,128)(2,1)}) %all-gather.7.cloned.1.call-update) | async-done | bytes 4194320 | tf_op jit(solution)/shard_map/all_gather | solution.py:33
  232.7 5.0 %multiply_reduce_fusion.2 = (f32[128]{0:T(128)S(1)}, f32[]{:T(128)}, f32[]{:T(128)}, f32[]{:T(128)}) fusion(f32[128,256]{1,0:T(8,128)S(1)} %fusion.3, bf16[128,8192]{1,0:T(8,128)(2,1)} %all-gather.5.cloned.1.call-done, bf16[256,8192]{1,0:T(8,128)(2,1)} %all-gather.7.cloned.1.call-done), kind=kOutput, calls=%fused_computation.8 | convolution fusion | flops 537100160 | bytes 6423052 | tf_op jit(solution)/shard_map/dot_general | solution.py:9
  237.7 39.6 %all-reduce.1 = (f32[]{:T(128)}, f32[]{:T(128)}, f32[]{:T(128)}) all-reduce(f32[]{:T(128)} %get-tuple-element.5, f32[]{:T(128)} %get-tuple-element.7, f32[]{:T(128)} %get-tuple-element.6), channel_id=1, replica_groups=mesh['gx'=8,'gy'=4] {'gx','gy'}, use_global_device_ids=true, to_apply=%region_4.0 | all-reduce | flops 3 | bytes 24 | tf_op jit(solution)/shard_map/psum | solution.py:37
  278.7 10.6 %all-reduce = f32[128]{0:T(128)S(1)} all-reduce(f32[128]{0:T(128)S(1)} %get-tuple-element.4), channel_id=2, replica_groups=mesh['gx'=8,'gy'=4] {'gy'}, use_global_device_ids=true, to_apply=%region_10.0.clone | all-reduce | flops 128 | bytes 1024
  290.0 0.6 fusion.2
  (2 shorter events, 0.0 us)
Async XLA Ops:
  7.2 78.2 %copy-start = (u32[32]{0:T(128)S(1)}, u32[32]{0:T(128)}, u32[]{:S(2)}) copy-start(u32[32]{0:T(128)} %constant.11) | copy-start | bytes 388
  7.2 101.8 %all-gather.9.cloned.1.call-start = ((), (), s32[]{:S(2)}) async-start(), calls=%async_computation.3 | async-start | bytes 2621440 | tf_op jit(solution)/shard_map/all_gather | solution.py:28
  52.5 94.6 %all-gather.11.cloned.1.call-start = ((), (), s32[]{:S(2)}) async-start(), calls=%async_computation.4 | async-start | bytes 4718592 | tf_op jit(solution)/shard_map/all_gather | solution.py:34
  53.3 141.7 %all-gather.5.cloned.1.call-start = ((), (), s32[]{:S(2)}) async-start(), calls=%async_computation.1 | async-start | bytes 2621440 | tf_op jit(solution)/shard_map/all_gather | solution.py:27
  84.7 147.9 %all-gather.7.cloned.1.call-start = ((), (), s32[]{:S(2)}) async-start(), calls=%async_computation.2 | async-start | bytes 4718592 | tf_op jit(solution)/shard_map/all_gather | solution.py:33
Sparse Core Ops, SparseCore 0:
  52.6 56.3 all-gather.8
  111.5 35.5 all-gather.10
  149.3 45.6 all-gather.4
  197.3 35.3 all-gather.6
where the time goes:
time: 299 us; the launch traced here: 298 us
  waiting for transfers between devices  143 us (48%)
  blocking collectives  121 us (40%)
  between operations  17.6 us (6%)
  matrix products  9.4 us (3%)
  other arithmetic  6.03 us (2%)
    all_gather x1, waiting for transfers between devices, body(): lax.all_gather(early_rows, 'gy', axis=0, tiled=True)  43.5 us
    psum x1, blocking collectives, body(): column_sums = lax.psum(jnp.sum(late_values, axis=0), ('gx', 'gy'))  42.1 us
    psum x1, blocking collectives, body(): lax.psum((jnp.sum(row_part), early_part, late_part), ('gx', 'gy'))  39.6 us
    all_gather x1, waiting for transfers between devices, body(): lax.all_gather(late_rows, 'gx', axis=0, tiled=True)  38.1 us
    all_gather x1, waiting for transfers between devices, body(): lax.all_gather(early_rows, 'gx', axis=0, tiled=True)  37.7 us
    all_to_all x1, blocking collectives, body(): lax.all_to_all(early_cols, ('gx', 'gy'), split_axis=0, concat_axis=1, til...  28.2 us
    all_gather x1, waiting for transfers between devices, body(): lax.all_gather(late_rows, 'gy', axis=0, tiled=True)  22.4 us
    unnamed x1, blocking collectives  10.6 us
  transfers between devices with their start and end apart: 4, of which 4 were waited for; matrix products, arithmetic and copies ran while one was open for 3% of the time, Pallas kernels for 0%

commit v1 on v0

--- a/solution.py
+++ b/solution.py
@@ -31,7 +31,15 @@
         block_early,
         block_late,
         lax.all_gather(early_rows, "gx", axis=0, tiled=True),
-        lax.all_gather(late_rows, "gx", axis=0, tiled=True),
+        jnp.concatenate(
+            lax.all_to_all(
+                jnp.stack([late_rows for _ in range(lax.axis_size("gx"))], axis=0),
+                concat_axis=0,
+                split_axis=0,
+                axis_name="gx",
+            ),
+            axis=0,
+        ),
     )
     own_align = lax.psum_scatter(row_part, "gy", scatter_dimension=0, tiled=True)
     total_kl, total_kk, total_ll = lax.psum(

time: 299 us -> 259 us (0.87)
  waiting for transfers between devices: 143 us -> 95.1 us
  starting transfers between devices: 0.16 us -> 6.65 us
    all_gather x1 -> x0, waiting for transfers between devices: 38.1 us -> none  [body(): lax.all_gather(late_rows, 'gx', axis=0, tiled=True)]
    all_gather x1, waiting for transfers between devices: 43.5 us -> 7.98 us  [body(): lax.all_gather(early_rows, 'gy', axis=0, tiled=True)]
    all_to_all x0 -> x1, waiting for transfers between devices: none -> 34.4 us  [body(): lax.all_to_all(jnp.stack([late_rows for _ in range(lax.axis_size('gx'))],...]
    all_gather x1, waiting for transfers between devices: 22.4 us -> 14 us  [body(): lax.all_gather(late_rows, 'gy', axis=0, tiled=True)]
    all_to_all x0 -> x1, starting transfers between devices: none -> 6.53 us  [body(): lax.all_to_all(jnp.stack([late_rows for _ in range(lax.axis_size('gx'))],...]
  transfers between devices with their start and end apart: 4 -> 4, of which waited for: 4 -> 4; matrix products, arithmetic and copies ran while one was open for 3% -> 4% of each run, Pallas kernels for 0% -> 0%
where the time goes in v1:
time: 259 us
  blocking collectives  120 us (46%)
  waiting for transfers between devices  95.1 us (37%)
  between operations  17.6 us (7%)
  matrix products  9.42 us (4%)
  starting transfers between devices  6.65 us (3%)
  other arithmetic  6.07 us (2%)
  local copies, waits for them, and re-layouts  3.87 us (1%)
    psum x1, blocking collectives, body(): column_sums = lax.psum(jnp.sum(late_values, axis=0), ('gx', 'gy'))  42.1 us
    psum x1, blocking collectives, body(): lax.psum((jnp.sum(row_part), early_part, late_part), ('gx', 'gy'))  39.6 us
    all_gather x1, waiting for transfers between devices, body(): lax.all_gather(early_rows, 'gx', axis=0, tiled=True)  37.9 us
    all_to_all x1, waiting for transfers between devices, body(): lax.all_to_all(jnp.stack([late_rows for _ in range(lax.axis_size('gx'))],...  34.4 us
    all_to_all x1, blocking collectives, body(): lax.all_to_all(early_cols, ('gx', 'gy'), split_axis=0, concat_axis=1, til...  27.6 us
    all_gather x1, waiting for transfers between devices, body(): lax.all_gather(late_rows, 'gy', axis=0, tiled=True)  14 us
    unnamed x1, blocking collectives  10.6 us
    all_gather x1, waiting for transfers between devices, body(): lax.all_gather(early_rows, 'gy', axis=0, tiled=True)  7.98 us
  transfers between devices with their start and end apart: 4, of which 4 were waited for; matrix products, arithmetic and copies ran while one was open for 4% of the time, Pallas kernels for 0%

profile of v1, /device:TPU:0, one launch (start us, length us, event | category | flops | bytes accessed | tf_op | source)
XLA Modules:
  0.0 258.6 jit_solution(11675752291317669171)
XLA Ops:
  7.2 0.0 all-gather.8.cloned.1.call-start
  7.2 1.2 convert_reduce_fusion
  8.4 42.1 %psum.28 = f32[8192]{0:T(1024)S(1)} all-reduce(f32[8192]{0:T(1024)S(1)} %convert_reduce_fusion), channel_id=1, replica_groups=mesh['gx'=8,'gy'=4] {'gx','gy'}, use_global_device_ids=true, to_apply=%region_2.0 | all-reduce | flops 8192 | bytes 65536 | tf_op jit(solution)/shard_map/psum | solution.py:23
  50.5 1.9 fusion.1
  52.5 0.0 copy-start
  52.5 0.0 all-gather.8.cloned.1.call-update
  52.5 0.0 all-gather.4.cloned.1.call-start
  52.5 1.2 convert_reduce_fusion.1
  53.8 1.1 fusion
  54.9 27.6 %all_to_all.24 = bf16[32,32,256]{2,1,0:T(8,128)(2,1)S(1)} all-to-all(bf16[32,32,256]{2,1,0:T(8,128)(2,1)S(1)} %bitcast.13), channel_id=1, replica_groups=mesh['gx'=8,'gy'=4] {'gx','gy'}, dimensions={0} | all-to-all | bytes 1048576 | tf_op jit(solution)/shard_map/all_to_all | solution.py:25
  82.5 0.8 copy.8
  83.3 0.0 all-gather.4.cloned.1.call-update
  83.3 0.0 all-gather.6.cloned.1.call-start
  83.4 0.7 all-gather.6.cloned.1.call-update
  84.1 0.0 copy-done
  84.1 2.5 stack.2
  86.5 0.0 copy-start.1
  86.5 6.5 %all-to-all-start.1 = ((bf16[8,32,8192]{2,1,0:T(8,128)(2,1)}), bf16[8,32,8192]{2,1,0:T(8,128)(2,1)}, u32[]{:S(2)}, u32[]{:S(2)}) async-start(bf16[8,32,8192]{2,1,0:T(8,128)(2,1)} %stack.2), calls=%async_computation.1 | async-start | bytes 8388608 | tf_op jit(solution)/shard_map/all_to_all | solution.py:35
  93.1 0.0 copy-done.1
  93.1 0.6 dynamic-slice
  94.3 14.0 %all-gather.8.cloned.1.call-done = bf16[128,8192]{1,0:T(8,128)(2,1)} async-done(((bf16[32,8192]{1,0:T(8,128)(2,1)}), bf16[128,8192]{1,0:T(8,128)(2,1)}) %all-gather.8.cloned.1.call-update) | async-done | bytes 2097168 | tf_op jit(solution)/shard_map/all_gather | solution.py:28
  108.3 34.4 %all-to-all-done.1 = bf16[8,32,8192]{2,1,0:T(8,128)(2,1)} async-done(((bf16[8,32,8192]{2,1,0:T(8,128)(2,1)}), bf16[8,32,8192]{2,1,0:T(8,128)(2,1)}, u32[]{:S(2)}, u32[]{:S(2)}) %all-to-all-start.1) | async-done | bytes 4194336 | tf_op jit(solution)/shard_map/all_to_all | solution.py:35
  142.8 4.4 %fusion.3 = f32[128,256]{1,0:T(8,128)S(1)} fusion(bf16[128,8192]{1,0:T(8,128)(2,1)} %all-gather.8.cloned.1.call-done, bf16[256,8192]{1,0:T(8,128)(2,1)} %bitcast.2), kind=kOutput, calls=%fused_computation.14 | convolution fusion | flops 536870912 | bytes 6422528 | tf_op jit(solution)/shard_map/dot_general | solution.py:10
  147.2 8.0 %all-gather.4.cloned.1.call-done = bf16[128,8192]{1,0:T(8,128)(2,1)} async-done(((bf16[32,8192]{1,0:T(8,128)(2,1)}), bf16[128,8192]{1,0:T(8,128)(2,1)}) %all-gather.4.cloned.1.call-update) | async-done | bytes 2097168 | tf_op jit(solution)/shard_map/all_gather | solution.py:27
  155.1 37.9 %all-gather.6.cloned.1.call-done = bf16[256,8192]{1,0:T(8,128)(2,1)} async-done(((bf16[32,8192]{1,0:T(8,128)(2,1)}), bf16[256,8192]{1,0:T(8,128)(2,1)}) %all-gather.6.cloned.1.call-update) | async-done | bytes 4194320 | tf_op jit(solution)/shard_map/all_gather | solution.py:33
  193.0 5.0 %multiply_reduce_fusion.2 = (f32[128]{0:T(128)S(1)}, f32[]{:T(128)}, f32[]{:T(128)}, f32[]{:T(128)}) fusion(f32[128,256]{1,0:T(8,128)S(1)} %fusion.3, bf16[128,8192]{1,0:T(8,128)(2,1)} %all-gather.4.cloned.1.call-done, bf16[256,8192]{1,0:T(8,128)(2,1)} %all-gather.6.cloned.1.call-done), kind=kOutput, calls=%fused_computation.8 | convolution fusion | flops 537100160 | bytes 6423052 | tf_op jit(solution)/shard_map/dot_general | solution.py:9
  198.1 39.6 %all-reduce.1 = (f32[]{:T(128)}, f32[]{:T(128)}, f32[]{:T(128)}) all-reduce(f32[]{:T(128)} %get-tuple-element.5, f32[]{:T(128)} %get-tuple-element.7, f32[]{:T(128)} %get-tuple-element.6), channel_id=1, replica_groups=mesh['gx'=8,'gy'=4] {'gx','gy'}, use_global_device_ids=true, to_apply=%region_4.0 | all-reduce | flops 3 | bytes 24 | tf_op jit(solution)/shard_map/psum | solution.py:45
  239.0 10.6 %all-reduce = f32[128]{0:T(128)S(1)} all-reduce(f32[128]{0:T(128)S(1)} %get-tuple-element.4), channel_id=2, replica_groups=mesh['gx'=8,'gy'=4] {'gy'}, use_global_device_ids=true, to_apply=%region_10.0.clone | all-reduce | flops 128 | bytes 1024
  250.3 0.6 fusion.2
  (2 shorter events, 0.0 us)
Async XLA Ops:
  7.2 101.2 %all-gather.8.cloned.1.call-start = ((), (), s32[]{:S(2)}) async-start(), calls=%async_computation.4 | async-start | bytes 2621440 | tf_op jit(solution)/shard_map/all_gather | solution.py:28
  52.5 31.6 %copy-start = (bf16[32,8192]{1,0:T(8,128)(2,1)S(1)}, bf16[32,8192]{1,0:T(8,128)(2,1)}, u32[]{:S(2)}) copy-start(bf16[32,8192]{1,0:T(8,128)(2,1)} %fusion.1) | copy-start | bytes 1572868
  52.5 102.7 %all-gather.4.cloned.1.call-start = ((), (), s32[]{:S(2)}) async-start(), calls=%async_computation.2 | async-start | bytes 2621440 | tf_op jit(solution)/shard_map/all_gather | solution.py:27
  83.3 109.7 %all-gather.6.cloned.1.call-start = ((), (), s32[]{:S(2)}) async-start(), calls=%async_computation.3 | async-start | bytes 4718592 | tf_op jit(solution)/shard_map/all_gather | solution.py:33
  86.5 6.5 %copy-start.1 = (u32[32]{0:T(128)S(1)}, u32[32]{0:T(128)}, u32[]{:S(2)}) copy-start(u32[32]{0:T(128)} %constant.11) | copy-start | bytes 388
  86.5 56.2 %all-to-all-start.1 = ((bf16[8,32,8192]{2,1,0:T(8,128)(2,1)}), bf16[8,32,8192]{2,1,0:T(8,128)(2,1)}, u32[]{:S(2)}, u32[]{:S(2)}) async-start(bf16[8,32,8192]{2,1,0:T(8,128)(2,1)} %stack.2), calls=%async_computation.1 | async-start | bytes 8388608 | tf_op jit(solution)/shard_map/all_to_all | solution.py:35
Sparse Core Ops, SparseCore 0:
  52.6 55.6 all-gather.7
  110.5 44.6 all-gather.3
  157.6 35.3 all-gather.5
